TPU v7x, 32 devices: a whole 2x2x4 slice. The times are simulated.
32 devices in a mesh: grp: 2 (over y), seq: 16 (over z, x, core).
Axes of the slice: x: 2, y: 2, z: 4, core: 2. Of those that a mesh axis runs over, the one named last changes fastest.
Arguments:
- frames: bfloat16 [4, 10240, 1280], P('grp', 'seq'), parts along dimension 0, may hold values from -120 to 120
- dec_states: bfloat16 [2, 256, 1280], P(None, 'grp'), parts along dimension 1, may hold values from -6 to 6
- w_query: bfloat16 [1280, 1280], P(None, 'seq'), may hold values from -0.15625 to 0.15625
- w_keyval: bfloat16 [1280, 2560], replicated, may hold values from -0.15625 to 0.15625
- w_output: bfloat16 [1280, 1280], P(None, 'seq'), may hold values from -0.15625 to 0.15625
- head_slope: float32 [20], replicated, may hold values from 0.3 to 12
- lengths: int32 [4, 16], P('grp'), parts along dimension 0, may hold values from 128 to 640, as said below
- positions: int32 [2, 256], P(None, 'grp'), parts along dimension 1, may hold values from 0 to 15
Outputs:
- attended: bfloat16 [2, 256, 1280], P(None, 'grp', 'seq'), parts along dimension 1
There are 2 independent parts, one for each index of `grp`. A program takes and returns all parts, laid end to end along the dimension named above; an argument that names none is the same for every part. Nothing has to cross between parts.
Inputs may be any that keep to these rules, and one draw needn't show every extreme that they name: `lengths`: every step has one block of exactly 640 valid frames.
All inputs are finite; a program needn't handle non-finite values.
Results may differ from a plain program's by a relative error of at most 0.005.
The roundings to bfloat16 on the way count: a program that leaves them out, or rounds other values in their place, can miss the bound.
Values may be sent and summed in bfloat16 or wider, within the bound.
A program may use at most 128 MiB of HBM per device.

v0:
```python
import functools
import math
import jax
import jax.numpy as jnp
from jax import lax
from jax.sharding import PartitionSpec as P


def block_partial(
    queries,
    block_keys,
    block_values,
    length_now,
    slot_place,
    age_steps,
    row_positions,
    head_slope,
    devices,
):
    query_rows, head_count, head_size = queries.shape
    frame_count = block_keys.shape[0]
    keys_split = block_keys.reshape(frame_count, head_count, head_size)
    scores = jnp.einsum(
        "qhd,jhd->hqj", queries, keys_split, preferred_element_type=jnp.float32
    ) / math.sqrt(head_size)
    distance = (
        jnp.abs(row_positions.astype(jnp.float32) - slot_place.astype(jnp.float32)) / devices
        + age_steps
    )
    scores = scores - head_slope[:, None, None] * distance[None, :, None]
    valid = lax.broadcasted_iota(jnp.int32, (1, 1, frame_count), 2) < length_now
    scores = jnp.where(valid, scores, -jnp.inf)
    row_peak = jnp.max(scores, axis=2)
    weights = jnp.exp(scores - row_peak[:, :, None]).astype(jnp.bfloat16)
    row_total = jnp.sum(weights.astype(jnp.float32), axis=2)
    values_split = block_values.reshape(frame_count, head_count, head_size)
    row_context = jnp.einsum(
        "hqj,jhd->qhd", weights, values_split, preferred_element_type=jnp.float32
    )
    return (row_peak.T, row_total.T, row_context.reshape(query_rows, head_count * head_size))


def rescale(row_context, factors, head_count):
    query_rows = row_context.shape[0]
    spread_rows = row_context.reshape(query_rows, head_count, -1) * factors[:, :, None]
    return spread_rows.reshape(query_rows, -1)


def combine_parts(head_count, earlier, later):
    peak_one, total_one, context_one = earlier
    peak_two, total_two, context_two = later
    row_top = jnp.maximum(peak_one, peak_two)
    scale_one = jnp.exp(peak_one - row_top)
    scale_two = jnp.exp(peak_two - row_top)
    merged_total = total_one * scale_one + total_two * scale_two
    merged_context = rescale(context_one, scale_one, head_count) + rescale(
        context_two, scale_two, head_count
    )
    return (row_top, merged_total, merged_context)


def local(frames, dec_states, w_query, w_keyval, w_output, head_slope, lengths, positions):
    devices = lax.axis_size("seq")
    own_index = lax.axis_index("seq")
    step_count, frame_count, model_width = frames.shape
    query_rows = dec_states.shape[1]
    head_count = head_slope.shape[0]
    head_size = model_width // head_count
    frame_rows = frames.reshape(step_count * frame_count, model_width)
    keyval = jnp.dot(frame_rows, w_keyval, preferred_element_type=jnp.float32).astype(jnp.bfloat16)
    block_keys = keyval[:, :model_width].reshape(step_count, frame_count, model_width)
    block_values = keyval[:, model_width:].reshape(step_count, frame_count, model_width)
    dec_rows = dec_states.reshape(step_count * query_rows, model_width)
    local_query = jnp.dot(dec_rows, w_query, preferred_element_type=jnp.float32).astype(
        jnp.bfloat16
    )
    queries = lax.all_gather(local_query, "seq", axis=1, tiled=True)
    queries = queries.reshape(step_count, query_rows, head_count, head_size)
    combine = functools.partial(combine_parts, head_count)
    slot_place = (own_index + 1) % devices
    results = []
    for step_now in range(step_count):
        running = None
        for older_step in range(step_now + 1):
            partial_now = block_partial(
                queries[step_now],
                block_keys[older_step],
                block_values[older_step],
                lengths[older_step, own_index],
                slot_place,
                float(step_now - older_step),
                positions[step_now],
                head_slope,
                devices,
            )
            running = partial_now if running is None else combine(running, partial_now)
        row_peak, row_total, row_context = running
        row_top = lax.pmax(row_peak, "seq")
        factors = jnp.exp(row_peak - row_top)
        row_total, row_context = lax.psum(
            (row_total * factors, rescale(row_context, factors, head_count)), "seq"
        )
        context = row_context.reshape(query_rows, head_count, head_size) / row_total[:, :, None]
        context = context.reshape(query_rows, model_width).astype(jnp.bfloat16)
        results.append(
            jnp.dot(context, w_output, preferred_element_type=jnp.float32).astype(jnp.bfloat16)
        )
    return jnp.stack(results)


def solution(mesh):
    return jax.shard_map(
        local,
        mesh=mesh,
        in_specs=(
            P("grp", "seq", None),
            P(None, "grp", None),
            P(None, "seq"),
            P(),
            P(None, "seq"),
            P(),
            P("grp", None),
            P(None, "grp"),
        ),
        out_specs=P(None, "grp", "seq"),
        check_vma=False,
    )
```

profile of v0, /device:TPU:0, one launch (start us, length us, event | category | flops | bytes accessed | tf_op | source)
XLA Modules:
  0.0 259.9 jit_solution(2014881977530584230)
XLA Ops:
  6.5 0.0 copy-start
  6.5 0.0 all-reduce.5.cloned.1.call-start
  6.5 0.8 broadcast_add_fusion
  7.4 0.8 multiply_bitcast_fusion.1
  8.2 1.4 constant_dynamic-slice_fusion.1
  9.6 0.6 iota_compare_fusion.1
  10.3 0.0 copy-done
  10.3 10.8 %convolution_convert_fusion = bf16[1280,2560]{1,0:T(8,128)(2,1)S(1)} fusion(bf16[1280,1280]{1,0:T(8,128)(2,1)S(1)} %bitcast.89, bf16[1280,2560]{1,0:T(8,128)(2,1)} %param.11), kind=kOutput, calls=%fused_computation | convolution fusion | flops 8391884800 | bytes 16384000 | tf_op jit(solution)/shard_map/dot_general | solution.py:70
  21.1 0.0 copy-start.10
  21.1 2.8 %fusion.18 = (bf16[640,1280]{1,0:T(8,128)(2,1)}, bf16[640,1280]{1,0:T(8,128)(2,1)}, bf16[640,1280]{1,0:T(8,128)(2,1)}, bf16[640,1280]{1,0:T(8,128)(2,1)}) fusion(bf16[1280,2560]{1,0:T(8,128)(2,1)S(1)} %convolution_convert_fusion), kind=kLoop, calls=%fused_computation.53 | loop fusion | bytes 13107200 | tf_op jit(solution)/shard_map/slice | solution.py:88
  23.9 3.5 %copy.16 = bf16[640,1280]{0,1:T(8,128)(2,1)} copy(bf16[640,1280]{1,0:T(8,128)(2,1)} %get-tuple-element.26) | data formatting | bytes 3276800 | tf_op jit(solution)/shard_map/slice | solution.py:87
  27.4 0.0 copy-done.10
  27.4 1.4 convolution_convert_fusion.1
  28.9 25.1 %all_gather.3 = bf16[256,1280]{0,1:T(8,128)(2,1)S(1)} all-gather(bf16[256,80]{0,1:T(8,128)(2,1)S(1)} %convolution_convert_fusion.1), channel_id=1, replica_groups=mesh['grp'=2,'seq'=16] {'seq'}, dimensions={1}, use_global_device_ids=true | all-gather | bytes 696320 | tf_op jit(solution)/shard_map/all_gather | solution.py:77
  54.0 0.0 copy-start.11
  54.0 0.9 fusion.19
  54.9 0.6 iota_compare_fusion
  55.5 3.5 %copy.17 = bf16[640,1280]{0,1:T(8,128)(2,1)} copy(bf16[640,1280]{1,0:T(8,128)(2,1)} %get-tuple-element.25) | data formatting | bytes 3276800 | tf_op jit(solution)/shard_map/slice | solution.py:87
  59.1 0.0 copy-start.6
  59.1 0.0 copy-start.7
  59.1 2.7 %fusion.20 = f32[20,128,640]{2,1,0:T(8,128)S(1)} fusion(bf16[128,20,64]{0,2,1:T(8,128)(2,1)} %bitcast.98, bf16[640,20,64]{0,2,1:T(8,128)(2,1)} %bitcast.92), kind=kOutput, calls=%fused_computation.55 | convolution fusion | flops 209715200 | bytes 8519680 | tf_op jit(solution)/shard_map/qhd,jhd->hqj/dot_general | solution.py:23
  61.8 0.0 copy-start.1
  61.8 0.0 copy-start.3
  61.8 0.0 copy-start.9
  61.9 0.0 copy-done.11
  61.9 0.1 broadcast_multiply_fusion.1
  61.9 0.0 copy-done.6
  61.9 0.0 copy-done.7
  61.9 1.6 fusion.2
  63.5 0.0 copy-start.2
  63.5 1.0 copy-done.3
  64.5 0.3 copy-done.9
  64.8 4.6 %fusion = (f32[20,128]{1,0:T(8,128)S(1)}, f32[20,128]{1,0:T(8,128)S(1)}, f32[20,128,640]{2,1,0:T(8,128)}) fusion(f32[20,128]{1,0:T(8,128)S(1)} %get-tuple-element.33, pred[640]{0:T(1024)(128)(4,1)S(1)} %iota_compare_fusion.1, f32[20,128]{1,0:T(8,128)S(1)} %get-tuple-element.31, f32[20,128,640]{2,1,0:T(8,128)S(1)} %fusion.20, ...), kind=kOutput, calls=%fused_computation.10 | convolution fusion | flops 222817280 | bytes 15114880 | tf_op jit(solution)/shard_map/qhd,jhd->hqj/dot_general | solution.py:23
  69.4 0.0 copy-done.1
  69.4 0.0 copy-done.2
  69.4 2.0 convert_reduce_fusion
  71.4 3.5 %copy.15 = bf16[640,1280]{0,1:T(8,128)(2,1)} copy(bf16[640,1280]{1,0:T(8,128)(2,1)} %get-tuple-element.23) | data formatting | bytes 3276800 | tf_op jit(solution)/shard_map/slice | solution.py:88
  74.9 3.5 %copy.18 = bf16[640,1280]{0,1:T(8,128)(2,1)} copy(bf16[640,1280]{1,0:T(8,128)(2,1)} %get-tuple-element.24) | data formatting | bytes 3276800 | tf_op jit(solution)/shard_map/slice | solution.py:88
  78.4 7.1 %convert_reduce_fusion.2 = (f32[20,128]{1,0:T(8,128)S(1)}, f32[20,128]{1,0:T(8,128)S(1)}) fusion(f32[20,128]{1,0:T(8,128)S(1)} %get-tuple-element.7, f32[20,128]{1,0:T(8,128)S(1)} %get-tuple-element.33, f32[20,128,640]{2,1,0:T(8,128)} %get-tuple-element.36, pred[640]{0:T(1024)(128)(4,1)S(1)} %iota_compare_fusion.1, f32[20,128]{1,0:T(8,128)S(1)} %get-tuple-element.8, ...), kind=kLoop, calls=%fused_computation.7 | loop fusion | flops 22932480 | bytes 13169280 | tf_op jit(solution)/shard_map/reduce_sum | solution.py:35
  85.5 57.8 %all-reduce.2 = (f32[128,20]{0,1:T(8,128)S(1)}, f32[128,20]{0,1:T(8,128)S(1)}) all-reduce(f32[128,20]{0,1:T(8,128)S(1)} %bitcast_maximum_fusion, f32[128,20]{0,1:T(8,128)S(1)} %bitcast.104), channel_id=1, replica_groups=mesh['grp'=2,'seq'=16] {'seq'}, use_global_device_ids=true, to_apply=%region_7.8 | all-reduce | flops 5120 | bytes 40960 | tf_op jit(solution)/shard_map/pmax | solution.py:98
  143.3 0.0 copy-start.5
  143.4 6.2 %fusion.3 = f32[128,20,64]{0,2,1:T(8,128)} fusion(bf16[640,20,64]{0,2,1:T(8,128)(2,1)} %bitcast.94, f32[128,20]{0,1:T(8,128)S(1)} %get-tuple-element.38, f32[20,128,640]{2,1,0:T(8,128)} %get-tuple-element.36, f32[20,128]{1,0:T(8,128)S(1)} %get-tuple-element.7, f32[20,128]{1,0:T(8,128)S(1)} %get-tuple-element.33, pred[640]{0:T(1024)(128)(4,1)S(1)} %iota_compare_fusion.1), kind=kOutput, calls=%fused_computation.16 | convolution fusion | flops 218071040 | bytes 8878720 | tf_op jit(solution)/shard_map/hqj,jhd->qhd/dot_general | solution.py:37
  149.6 0.0 slice-start
  149.6 0.0 copy-start.4
  149.6 0.0 copy-done.5
  149.6 0.0 slice-start.1
  149.6 4.3 %fusion.7 = f32[128,20,64]{0,2,1:T(8,128)S(1)} fusion(bf16[640,20,64]{0,2,1:T(8,128)(2,1)S(1)} %bitcast.96, f32[128,20]{0,1:T(8,128)S(1)} %get-tuple-element.20, f32[20,128,640]{2,1,0:T(8,128)} %copy-done.2, f32[20,128]{1,0:T(8,128)S(1)} %get-tuple-element.34, f32[20,128]{1,0:T(8,128)S(1)} %get-tuple-element.32, pred[640]{0:T(1024)(128)(4,1)S(1)} %iota_compare_fusion), kind=kOutput, calls=%fused_computation.20 | convolution fusion | flops 218071040 | bytes 8878720 | tf_op jit(solution)/shard_map/hqj,jhd->qhd/dot_general | solution.py:37
  153.9 0.0 slice-done
  153.9 0.3 copy-done.4
  154.2 0.7 slice-done.1
  154.9 0.0 copy-start.8
  154.9 2.9 %fusion.6 = f32[128,20,64]{0,2,1:T(8,128)} fusion(f32[128,20,64]{0,2,1:T(8,128)S(1)} %fusion.7, bf16[640,20,64]{0,2,1:T(8,128)(2,1)S(1)} %bitcast.95, f32[128,20]{0,1:T(8,128)S(1)} %get-tuple-element.19, f32[128,20]{0,1:T(8,128)S(1)} %get-tuple-element.18, f32[20,128,640]{2,1,0:T(8,128)S(1)} %bitcast.91, f32[20,128]{1,0:T(8,128)S(1)} %get-tuple-element.8, ...), kind=kOutput, calls=%fused_computation.19 | convolution fusion | flops 218398720 | bytes 9544320 | tf_op jit(solution)/shard_map/hqj,jhd->qhd/dot_general | solution.py:37
  157.9 0.0 all-reduce.5.cloned.1.call-update
  157.9 58.0 %all-reduce = (f32[128,20]{0,1:T(8,128)S(1)}, f32[128,20]{0,1:T(8,128)S(1)}) all-reduce(f32[128,20]{0,1:T(8,128)S(1)} %get-tuple-element.17, f32[128,20]{0,1:T(8,128)S(1)} %get-tuple-element.37), channel_id=1, replica_groups=mesh['grp'=2,'seq'=16] {'seq'}, use_global_device_ids=true, to_apply=%region_11.12 | all-reduce | flops 5120 | bytes 40960 | tf_op jit(solution)/shard_map/psum | solution.py:100
  215.9 33.8 %all-reduce.5.cloned.1.call-done = (f32[128,1280]{0,1:T(8,128)}, f32[128,1280]{0,1:T(8,128)}) async-done(((f32[128,1280]{0,1:T(8,128)}, f32[128,1280]{0,1:T(8,128)}), (f32[128,1280]{0,1:T(8,128)}, f32[128,1280]{0,1:T(8,128)})) %all-reduce.5.cloned.1.call-update) | async-done | bytes 1310736 | tf_op jit(solution)/shard_map/psum | solution.py:100
  249.7 1.1 fusion.11
  250.8 0.0 copy-done.8
  250.8 0.2 fusion.8
  251.0 1.1 fusion.10
  252.2 0.2 fusion.9
  252.4 0.6 pad_maximum_fusion
  (3 shorter events, 0.0 us)
Async XLA Ops:
  6.5 3.7 %copy-start = (bf16[2,640,1280]{2,1,0:T(8,128)(2,1)S(1)}, bf16[2,640,1280]{2,1,0:T(8,128)(2,1)}, u32[]{:S(2)}) copy-start(bf16[2,640,1280]{2,1,0:T(8,128)(2,1)} %param.8) | copy-start | bytes 9830404
  6.5 243.1 %all-reduce.5.cloned.1.call-start = ((), (), s32[]{:S(2)}) async-start(), calls=%async_computation | async-start | bytes 2621440 | tf_op jit(solution)/shard_map/psum | solution.py:100
  21.1 6.3 %copy-start.10 = (bf16[1280,80]{0,1:T(8,128)(2,1)S(1)}, bf16[1280,80]{0,1:T(8,128)(2,1)}, u32[]{:S(2)}) copy-start(bf16[1280,80]{0,1:T(8,128)(2,1)} %param.10) | copy-start | bytes 614404
  54.0 7.9 %copy-start.11 = (f32[20]{0:T(128)S(1)}, f32[20]{0:T(128)}, u32[]{:S(2)}) copy-start(f32[20]{0:T(128)} %param.13) | copy-start | bytes 244
  59.1 2.9 %copy-start.6 = (bf16[640,1280]{0,1:T(8,128)(2,1)S(1)}, bf16[640,1280]{0,1:T(8,128)(2,1)}, u32[]{:S(2)}) copy-start(bf16[640,1280]{0,1:T(8,128)(2,1)} %copy.17) | copy-start | bytes 4915204
  59.1 2.9 %copy-start.7 = (bf16[128,1280]{0,1:T(8,128)(2,1)S(1)}, bf16[128,1280]{0,1:T(8,128)(2,1)}, u32[]{:S(2)}) copy-start(bf16[128,1280]{0,1:T(8,128)(2,1)} %get-tuple-element.28) | copy-start | bytes 983044
  61.8 7.5 %copy-start.1 = (f32[20,128,640]{2,1,0:T(8,128)}, f32[20,128,640]{2,1,0:T(8,128)S(1)}, u32[]{:S(2)}) copy-start(f32[20,128,640]{2,1,0:T(8,128)S(1)} %fusion.20) | copy-start | bytes 19660804
  61.8 2.6 %copy-start.3 = (bf16[640,1280]{0,1:T(8,128)(2,1)S(1)}, bf16[640,1280]{0,1:T(8,128)(2,1)}, u32[]{:S(2)}) copy-start(bf16[640,1280]{0,1:T(8,128)(2,1)} %copy.16) | copy-start | bytes 4915204
  61.8 2.9 %copy-start.9 = (bf16[128,1280]{0,1:T(8,128)(2,1)S(1)}, bf16[128,1280]{0,1:T(8,128)(2,1)}, u32[]{:S(2)}) copy-start(bf16[128,1280]{0,1:T(8,128)(2,1)} %get-tuple-element.27) | copy-start | bytes 983044
  63.5 5.9 %copy-start.2 = (f32[20,128,640]{2,1,0:T(8,128)}, f32[20,128,640]{2,1,0:T(8,128)S(1)}, u32[]{:S(2)}) copy-start(f32[20,128,640]{2,1,0:T(8,128)S(1)} %get-tuple-element.35) | copy-start | bytes 19660804
  143.3 6.3 %copy-start.5 = (bf16[640,1280]{0,1:T(8,128)(2,1)S(1)}, bf16[640,1280]{0,1:T(8,128)(2,1)}, u32[]{:S(2)}) copy-start(bf16[640,1280]{0,1:T(8,128)(2,1)} %copy.18) | copy-start | bytes 4915204
  149.6 4.3 %slice-start = ((s8[6553600]{0:T(1024)(128)(4,1)}), s8[4194304]{0:T(1024)(128)(4,1)S(1)}, s32[]{:S(2)}) async-start(s8[6553600]{0:T(1024)(128)(4,1)} %bitcast.90), calls=%async_computation.1 | async-start | bytes 8388608
  149.6 4.6 %copy-start.4 = (bf16[640,1280]{0,1:T(8,128)(2,1)S(1)}, bf16[640,1280]{0,1:T(8,128)(2,1)}, u32[]{:S(2)}) copy-start(bf16[640,1280]{0,1:T(8,128)(2,1)} %copy.15) | copy-start | bytes 4915204
  149.6 5.3 %slice-start.1 = ((s8[6553600]{0:T(1024)(128)(4,1)}), s8[2359296]{0:T(1024)(128)(4,1)S(1)}, s32[]{:S(2)}) async-start(s8[6553600]{0:T(1024)(128)(4,1)} %bitcast.90), calls=%async_computation.2 | async-start | bytes 4718592
  154.9 95.9 %copy-start.8 = (bf16[1280,80]{0,1:T(8,128)(2,1)S(1)}, bf16[1280,80]{0,1:T(8,128)(2,1)}, u32[]{:S(2)}) copy-start(bf16[1280,80]{0,1:T(8,128)(2,1)} %param.12) | copy-start | bytes 614404
Sparse Core Ops, SparseCore 0:
  158.0 91.5 all-reduce.4
where the time goes:
time: 260 us
  blocking collectives  141 us (54%)
  matrix products  35 us (13%)
  waiting for transfers between devices  33.8 us (13%)
  local copies, waits for them, and re-layouts  21.6 us (8%)
  other arithmetic  15.1 us (6%)
  between operations  13.6 us (5%)
    psum x1, blocking collectives, local(): lax.psum((row_total * factors, rescale(row_context, factors, head_count))...  58 us
    pmax x1, blocking collectives, local(): row_top = lax.pmax(row_peak, 'seq')  57.8 us
    psum x1, waiting for transfers between devices, local(): lax.psum((row_total * factors, rescale(row_context, factors, head_count))...  33.8 us
    all_gather x1, blocking collectives, local(): queries = lax.all_gather(local_query, 'seq', axis=1, tiled=True)  25.1 us
    dot_general x3, matrix products, block_partial(): jnp.einsum('hqj,jhd->qhd', weights, values_split, preferred_element_type=...  13.5 us
    dot_general x1, matrix products, local(): jnp.dot(frame_rows, w_keyval, preferred_element_type=jnp.float32)  10.8 us
    slice x3, local copies, waits for them, and re-layouts, local(): block_values[older_step]  9.87 us
    reduce_sum x2, other arithmetic, block_partial(): row_total = jnp.sum(weights.astype(jnp.float32), axis=2)  9.08 us
  transfers between devices with their start and end apart: 1, of which 1 were waited for; matrix products, arithmetic and copies ran while one was open for 0% of the time, Pallas kernels for 0%

commit v1 on v0

--- a/solution.py
+++ b/solution.py
@@ -74,7 +74,9 @@
     local_query = jnp.dot(dec_rows, w_query, preferred_element_type=jnp.float32).astype(
         jnp.bfloat16
     )
-    queries = lax.all_gather(local_query, "seq", axis=1, tiled=True)
+    queries = jnp.concatenate(
+        lax.all_to_all(jnp.stack([local_query] * lax.axis_size("seq")), "seq", 0, 0), axis=1
+    )
     queries = queries.reshape(step_count, query_rows, head_count, head_size)
     combine = functools.partial(combine_parts, head_count)
     slot_place = (own_index + 1) % devices

time: 260 us -> 241 us (0.927)
  blocking collectives: 141 us -> 120 us
  starting transfers between devices: 0.01 us -> 7.47 us
  other arithmetic: 15.1 us -> 10.5 us
    all_gather x1 -> x0, blocking collectives: 25.1 us -> none  [local(): queries = lax.all_gather(local_query, 'seq', axis=1, tiled=True)]
    all_to_all x0 -> x1, starting transfers between devices: none -> 7.43 us  [local(): lax.all_to_all(jnp.stack([local_query] * lax.axis_size('seq')), 'seq', 0, 0)]
    pmax x1, blocking collectives: 57.8 us -> 61.8 us  [local(): row_top = lax.pmax(row_peak, 'seq')]
    reduce_sum x2, other arithmetic: 9.08 us -> 6.28 us  [block_partial(): row_total = jnp.sum(weights.astype(jnp.float32), axis=2)]
  transfers between devices with their start and end apart: 1 -> 2, of which waited for: 1 -> 1; matrix products, arithmetic and copies ran while one was open for 0% -> 12% of each run, Pallas kernels for 0% -> 0%
where the time goes in v1:
time: 241 us; the launch traced here: 240 us
  blocking collectives  120 us (50%)
  waiting for transfers between devices  33.8 us (14%)
  matrix products  33.3 us (14%)
  local copies, waits for them, and re-layouts  21.8 us (9%)
  between operations  13.6 us (6%)
  other arithmetic  10.5 us (4%)
  starting transfers between devices  7.47 us (3%)
    pmax x1, blocking collectives, local(): row_top = lax.pmax(row_peak, 'seq')  61.8 us
    psum x1, blocking collectives, local(): lax.psum((row_total * factors, rescale(row_context, factors, head_count))...  58 us
    psum x1, waiting for transfers between devices, local(): lax.psum((row_total * factors, rescale(row_context, factors, head_count))...  33.8 us
    dot_general x3, matrix products, block_partial(): jnp.einsum('hqj,jhd->qhd', weights, values_split, preferred_element_type=...  13.5 us
    dot_general x1, matrix products, local(): jnp.dot(frame_rows, w_keyval, preferred_element_type=jnp.float32)  10.8 us
    slice x3, local copies, waits for them, and re-layouts, local(): block_values[older_step]  9.86 us
    all_to_all x1, starting transfers between devices, local(): lax.all_to_all(jnp.stack([local_query] * lax.axis_size('seq')), 'seq', 0, 0)  7.43 us
    slice x2, local copies, waits for them, and re-layouts, local(): block_keys[older_step]  7.1 us
  transfers between devices with their start and end apart: 2, of which 1 were waited for; matrix products, arithmetic and copies ran while one was open for 12% of the time, Pallas kernels for 0%

profile of v1, /device:TPU:0, one launch (start us, length us, event | category | flops | bytes accessed | tf_op | source)
XLA Modules:
  0.0 240.2 jit_solution(14695571678892669176)
XLA Ops:
  6.5 0.0 copy-start
  6.5 1.6 convolution_convert_fusion.1
  8.2 0.9 stack.8
  9.1 7.4 %all-to-all-start = ((bf16[16,256,80]{1,2,0:T(8,128)(2,1)}), bf16[16,256,80]{1,2,0:T(8,128)(2,1)}, u32[]{:S(2)}, u32[]{:S(2)}) async-start(bf16[16,256,80]{1,2,0:T(8,128)(2,1)} %stack.8), calls=%async_computation | async-start | bytes 1310720 | tf_op jit(solution)/shard_map/all_to_all | solution.py:78
  16.5 0.0 all-reduce.5.cloned.1.call-start
  16.5 0.0 copy-done
  16.5 10.8 %convolution_convert_fusion = bf16[1280,2560]{1,0:T(8,128)(2,1)S(1)} fusion(bf16[1280,1280]{1,0:T(8,128)(2,1)S(1)} %bitcast.90, bf16[1280,2560]{1,0:T(8,128)(2,1)} %param.11), kind=kOutput, calls=%fused_computation | convolution fusion | flops 8391884800 | bytes 16384000 | tf_op jit(solution)/shard_map/dot_general | solution.py:70
  27.4 2.8 %fusion.18 = (bf16[640,1280]{1,0:T(8,128)(2,1)}, bf16[640,1280]{1,0:T(8,128)(2,1)}, bf16[640,1280]{1,0:T(8,128)(2,1)}, bf16[640,1280]{1,0:T(8,128)(2,1)}) fusion(bf16[1280,2560]{1,0:T(8,128)(2,1)S(1)} %convolution_convert_fusion), kind=kLoop, calls=%fused_computation.53 | loop fusion | bytes 13107200 | tf_op jit(solution)/shard_map/slice | solution.py:90
  30.2 0.0 copy-start.9
  30.2 0.0 copy-start.11
  30.2 0.0 copy-start.10
  30.2 3.6 %copy.16 = bf16[640,1280]{0,1:T(8,128)(2,1)} copy(bf16[640,1280]{1,0:T(8,128)(2,1)} %get-tuple-element.26) | data formatting | bytes 3276800 | tf_op jit(solution)/shard_map/slice | solution.py:89
  33.7 3.5 %copy.17 = bf16[640,1280]{0,1:T(8,128)(2,1)} copy(bf16[640,1280]{1,0:T(8,128)(2,1)} %get-tuple-element.25) | data formatting | bytes 3276800 | tf_op jit(solution)/shard_map/slice | solution.py:89
  37.3 3.5 %copy.15 = bf16[640,1280]{0,1:T(8,128)(2,1)} copy(bf16[640,1280]{1,0:T(8,128)(2,1)} %get-tuple-element.23) | data formatting | bytes 3276800 | tf_op jit(solution)/shard_map/slice | solution.py:90
  40.8 3.5 %copy.18 = bf16[640,1280]{0,1:T(8,128)(2,1)} copy(bf16[640,1280]{1,0:T(8,128)(2,1)} %get-tuple-element.24) | data formatting | bytes 3276800 | tf_op jit(solution)/shard_map/slice | solution.py:90
  44.3 0.0 copy-done.9
  44.3 0.6 constant_dynamic-slice_fusion.1
  44.9 0.6 iota_compare_fusion.1
  45.6 0.6 iota_compare_fusion
  46.1 0.0 copy-done.11
  46.2 0.0 copy-done.10
  46.2 0.1 broadcast_multiply_fusion.1
  46.3 0.0 all-to-all-done
  46.3 0.0 copy-start.7
  46.3 1.2 fusion.19
  47.5 2.5 %fusion.20 = f32[20,128,640]{2,1,0:T(8,128)S(1)} fusion(bf16[128,20,64]{0,2,1:T(8,128)(2,1)S(1)} %bitcast.99, bf16[640,20,64]{0,2,1:T(8,128)(2,1)} %bitcast.93), kind=kOutput, calls=%fused_computation.55 | convolution fusion | flops 209715200 | bytes 8519680 | tf_op jit(solution)/shard_map/qhd,jhd->hqj/dot_general | solution.py:23
  50.0 0.0 copy-start.1
  50.0 0.0 copy-start.4
  50.0 0.0 copy-done.7
  50.0 1.6 fusion.2
  51.6 0.0 copy-start.2
  51.6 1.0 copy-done.4
  52.6 2.9 %fusion = (f32[20,128]{1,0:T(8,128)S(1)}, f32[20,128]{1,0:T(8,128)S(1)}, f32[20,128,640]{2,1,0:T(8,128)S(1)}) fusion(f32[20,128]{1,0:T(8,128)S(1)} %get-tuple-element.33, pred[640]{0:T(1024)(128)(4,1)S(1)} %iota_compare_fusion.1, f32[20,128]{1,0:T(8,128)S(1)} %get-tuple-element.31, f32[20,128,640]{2,1,0:T(8,128)S(1)} %fusion.20, ...), kind=kOutput, calls=%fused_computation.10 | convolution fusion | flops 222817280 | bytes 15114880 | tf_op jit(solution)/shard_map/qhd,jhd->hqj/dot_general | solution.py:23
  55.5 0.0 copy-start.3
  55.6 0.0 copy-done.2
  55.6 2.0 convert_reduce_fusion
  57.6 0.0 copy-done.1
  57.6 4.3 %convert_reduce_fusion.2 = (f32[20,128]{1,0:T(8,128)S(1)}, f32[20,128]{1,0:T(8,128)S(1)}) fusion(f32[20,128]{1,0:T(8,128)S(1)} %get-tuple-element.7, f32[20,128]{1,0:T(8,128)S(1)} %get-tuple-element.33, f32[20,128,640]{2,1,0:T(8,128)S(1)} %get-tuple-element.36, pred[640]{0:T(1024)(128)(4,1)S(1)} %iota_compare_fusion.1, f32[20,128]{1,0:T(8,128)S(1)} %get-tuple-element.8, ...), kind=kLoop, calls=%fused_computation.7 | loop fusion | flops 22932480 | bytes 13169280 | tf_op jit(solution)/shard_map/reduce_sum | solution.py:35
  61.9 0.0 copy-done.3
  61.9 61.8 %all-reduce.2 = (f32[128,20]{0,1:T(8,128)S(1)}, f32[128,20]{0,1:T(8,128)S(1)}) all-reduce(f32[128,20]{0,1:T(8,128)S(1)} %bitcast_maximum_fusion, f32[128,20]{0,1:T(8,128)S(1)} %bitcast.105), channel_id=1, replica_groups=mesh['grp'=2,'seq'=16] {'seq'}, use_global_device_ids=true, to_apply=%region_7.8 | all-reduce | flops 5120 | bytes 40960 | tf_op jit(solution)/shard_map/pmax | solution.py:100
  123.7 0.0 copy-start.6
  123.7 6.2 %fusion.3 = f32[128,20,64]{0,2,1:T(8,128)} fusion(bf16[640,20,64]{0,2,1:T(8,128)(2,1)} %bitcast.95, f32[128,20]{0,1:T(8,128)S(1)} %get-tuple-element.38, f32[20,128,640]{2,1,0:T(8,128)} %copy-done.3, f32[20,128]{1,0:T(8,128)S(1)} %get-tuple-element.7, f32[20,128]{1,0:T(8,128)S(1)} %get-tuple-element.33, pred[640]{0:T(1024)(128)(4,1)S(1)} %iota_compare_fusion.1), kind=kOutput, calls=%fused_computation.16 | convolution fusion | flops 218071040 | bytes 8878720 | tf_op jit(solution)/shard_map/hqj,jhd->qhd/dot_general | solution.py:37
  130.0 0.0 slice-start
  130.0 0.0 copy-start.5
  130.0 0.0 copy-done.6
  130.0 0.0 slice-start.1
  130.0 4.3 %fusion.7 = f32[128,20,64]{0,2,1:T(8,128)S(1)} fusion(bf16[640,20,64]{0,2,1:T(8,128)(2,1)S(1)} %bitcast.97, f32[128,20]{0,1:T(8,128)S(1)} %get-tuple-element.20, f32[20,128,640]{2,1,0:T(8,128)} %copy-done.2, f32[20,128]{1,0:T(8,128)S(1)} %get-tuple-element.34, f32[20,128]{1,0:T(8,128)S(1)} %get-tuple-element.32, pred[640]{0:T(1024)(128)(4,1)S(1)} %iota_compare_fusion), kind=kOutput, calls=%fused_computation.20 | convolution fusion | flops 218071040 | bytes 8878720 | tf_op jit(solution)/shard_map/hqj,jhd->qhd/dot_general | solution.py:37
  134.3 0.0 slice-done
  134.3 0.3 copy-done.5
  134.6 0.7 slice-done.1
  135.3 0.0 copy-start.8
  135.3 3.0 %fusion.6 = f32[128,20,64]{0,2,1:T(8,128)} fusion(f32[128,20,64]{0,2,1:T(8,128)S(1)} %fusion.7, bf16[640,20,64]{0,2,1:T(8,128)(2,1)S(1)} %bitcast.96, f32[128,20]{0,1:T(8,128)S(1)} %get-tuple-element.19, f32[128,20]{0,1:T(8,128)S(1)} %get-tuple-element.18, f32[20,128,640]{2,1,0:T(8,128)S(1)} %bitcast.92, f32[20,128]{1,0:T(8,128)S(1)} %get-tuple-element.8, ...), kind=kOutput, calls=%fused_computation.19 | convolution fusion | flops 218398720 | bytes 9544320 | tf_op jit(solution)/shard_map/hqj,jhd->qhd/dot_general | solution.py:37
  138.3 0.0 all-reduce.5.cloned.1.call-update
  138.3 58.0 %all-reduce = (f32[128,20]{0,1:T(8,128)S(1)}, f32[128,20]{0,1:T(8,128)S(1)}) all-reduce(f32[128,20]{0,1:T(8,128)S(1)} %get-tuple-element.17, f32[128,20]{0,1:T(8,128)S(1)} %get-tuple-element.37), channel_id=1, replica_groups=mesh['grp'=2,'seq'=16] {'seq'}, use_global_device_ids=true, to_apply=%region_11.12 | all-reduce | flops 5120 | bytes 40960 | tf_op jit(solution)/shard_map/psum | solution.py:102
  196.3 33.8 %all-reduce.5.cloned.1.call-done = (f32[128,1280]{0,1:T(8,128)}, f32[128,1280]{0,1:T(8,128)}) async-done(((f32[128,1280]{0,1:T(8,128)}, f32[128,1280]{0,1:T(8,128)}), (f32[128,1280]{0,1:T(8,128)}, f32[128,1280]{0,1:T(8,128)})) %all-reduce.5.cloned.1.call-update) | async-done | bytes 1310736 | tf_op jit(solution)/shard_map/psum | solution.py:102
  230.0 1.1 fusion.11
  231.2 0.0 copy-done.8
  231.2 0.2 fusion.8
  231.4 1.1 fusion.10
  232.5 0.2 fusion.9
  232.8 0.6 pad_maximum_fusion
  (5 shorter events, 0.0 us)
Async XLA Ops:
  6.5 10.0 %copy-start = (bf16[2,640,1280]{2,1,0:T(8,128)(2,1)S(1)}, bf16[2,640,1280]{2,1,0:T(8,128)(2,1)}, u32[]{:S(2)}) copy-start(bf16[2,640,1280]{2,1,0:T(8,128)(2,1)} %param.8) | copy-start | bytes 9830404
  9.1 37.2 %all-to-all-start = ((bf16[16,256,80]{1,2,0:T(8,128)(2,1)}), bf16[16,256,80]{1,2,0:T(8,128)(2,1)}, u32[]{:S(2)}, u32[]{:S(2)}) async-start(bf16[16,256,80]{1,2,0:T(8,128)(2,1)} %stack.8), calls=%async_computation | async-start | bytes 1310720 | tf_op jit(solution)/shard_map/all_to_all | solution.py:78
  16.5 213.5 %all-reduce.5.cloned.1.call-start = ((), (), s32[]{:S(2)}) async-start(), calls=%async_computation.1 | async-start | bytes 2621440 | tf_op jit(solution)/shard_map/psum | solution.py:102
  30.2 14.1 %copy-start.9 = (s32[2,16]{1,0:T(2,128)S(1)}, s32[2,16]{1,0:T(2,128)}, u32[]{:S(2)}) copy-start(s32[2,16]{1,0:T(2,128)} %param.14) | copy-start | bytes 388
  30.2 15.9 %copy-start.11 = (s32[2,128]{1,0:T(2,128)S(1)}, s32[2,128]{1,0:T(2,128)}, u32[]{:S(2)}) copy-start(s32[2,128]{1,0:T(2,128)} %param.15) | copy-start | bytes 3076
  30.2 16.0 %copy-start.10 = (f32[20]{0:T(128)S(1)}, f32[20]{0:T(128)}, u32[]{:S(2)}) copy-start(f32[20]{0:T(128)} %param.13) | copy-start | bytes 244
  46.3 3.8 %copy-start.7 = (bf16[640,1280]{0,1:T(8,128)(2,1)S(1)}, bf16[640,1280]{0,1:T(8,128)(2,1)}, u32[]{:S(2)}) copy-start(bf16[640,1280]{0,1:T(8,128)(2,1)} %copy.17) | copy-start | bytes 4915204
  50.0 7.6 %copy-start.1 = (f32[20,128,640]{2,1,0:T(8,128)}, f32[20,128,640]{2,1,0:T(8,128)S(1)}, u32[]{:S(2)}) copy-start(f32[20,128,640]{2,1,0:T(8,128)S(1)} %fusion.20) | copy-start | bytes 19660804
  50.0 2.6 %copy-start.4 = (bf16[640,1280]{0,1:T(8,128)(2,1)S(1)}, bf16[640,1280]{0,1:T(8,128)(2,1)}, u32[]{:S(2)}) copy-start(bf16[640,1280]{0,1:T(8,128)(2,1)} %copy.16) | copy-start | bytes 4915204
  51.6 3.9 %copy-start.2 = (f32[20,128,640]{2,1,0:T(8,128)}, f32[20,128,640]{2,1,0:T(8,128)S(1)}, u32[]{:S(2)}) copy-start(f32[20,128,640]{2,1,0:T(8,128)S(1)} %get-tuple-element.35) | copy-start | bytes 19660804
  55.5 6.3 %copy-start.3 = (f32[20,128,640]{2,1,0:T(8,128)}, f32[20,128,640]{2,1,0:T(8,128)S(1)}, u32[]{:S(2)}) copy-start(f32[20,128,640]{2,1,0:T(8,128)S(1)} %get-tuple-element.36) | copy-start | bytes 19660804
  123.7 6.3 %copy-start.6 = (bf16[640,1280]{0,1:T(8,128)(2,1)S(1)}, bf16[640,1280]{0,1:T(8,128)(2,1)}, u32[]{:S(2)}) copy-start(bf16[640,1280]{0,1:T(8,128)(2,1)} %copy.18) | copy-start | bytes 4915204
  130.0 4.3 %slice-start = ((s8[6553600]{0:T(1024)(128)(4,1)}), s8[4194304]{0:T(1024)(128)(4,1)S(1)}, s32[]{:S(2)}) async-start(s8[6553600]{0:T(1024)(128)(4,1)} %bitcast.91), calls=%async_computation.2 | async-start | bytes 8388608
  130.0 4.6 %copy-start.5 = (bf16[640,1280]{0,1:T(8,128)(2,1)S(1)}, bf16[640,1280]{0,1:T(8,128)(2,1)}, u32[]{:S(2)}) copy-start(bf16[640,1280]{0,1:T(8,128)(2,1)} %copy.15) | copy-start | bytes 4915204
  130.0 5.3 %slice-start.1 = ((s8[6553600]{0:T(1024)(128)(4,1)}), s8[2359296]{0:T(1024)(128)(4,1)S(1)}, s32[]{:S(2)}) async-start(s8[6553600]{0:T(1024)(128)(4,1)} %bitcast.91), calls=%async_computation.3 | async-start | bytes 4718592
  135.3 95.9 %copy-start.8 = (bf16[1280,80]{0,1:T(8,128)(2,1)S(1)}, bf16[1280,80]{0,1:T(8,128)(2,1)}, u32[]{:S(2)}) copy-start(bf16[1280,80]{0,1:T(8,128)(2,1)} %param.12) | copy-start | bytes 614404
Sparse Core Ops, SparseCore 0:
  138.4 91.5 all-reduce.4
